TPU v7x, 32 devices: a whole 2x2x4 slice. The times are simulated.
32 devices in a mesh: dp: 4 (over z), row: 4 (over y, core), col: 2 (over x).
Axes of the slice: x: 2, y: 2, z: 4, core: 2. Of those that a mesh axis runs over, the one named last changes fastest.
Arguments:
- inputs: bfloat16 [16384, 1024], P(('dp', 'col'), 'row'), may hold values from -6 to 6
- gain_first: float32 [1024], P('row'), may hold values from 0.5 to 1.5
- shift_first: float32 [1024], P('row'), may hold values from -1 to 1
- w_query: bfloat16 [1024, 1024], P('row', 'col'), may hold values from -0.1875 to 0.1875
- w_key: bfloat16 [1024, 1024], P('row', 'col'), may hold values from -0.1875 to 0.1875
- w_value: bfloat16 [1024, 1024], P('row', 'col'), may hold values from -0.1875 to 0.1875
- w_output: bfloat16 [1024, 1024], P('col', 'row'), may hold values from -1.5 to 1.5
- gain_second: float32 [1024], P('row'), may hold values from 0.5 to 1.5
- shift_second: float32 [1024], P('row'), may hold values from -1 to 1
- w_up: bfloat16 [1024, 4096], P('row', 'col'), may hold values from -0.1875 to 0.1875
- bias_up: float32 [4096], P('col'), may hold values from -1.5 to 1.5
- w_down: bfloat16 [4096, 1024], P('col', 'row'), may hold values from -0.09375 to 0.09375
- bias_down: float32 [1024], P('row'), may hold values from -2.5 to 2.5
- segments: int32 [16, 1024], P(('dp', 'row')), may hold values from 0 to 4, as said below
- random_blocks: int32 [16, 16, 3], P('col'), may hold values from 0 to 15
- global_blocks: int32 [2], replicated, may hold values from 0 to 15, as said below
- cotangent: bfloat16 [16384, 1024], P(('dp', 'col'), 'row'), may hold values from -6 to 6
Outputs:
- layer_out: bfloat16 [16384, 1024], P(('dp', 'col'), 'row')
- grad_inputs: float32 [16384, 1024], P(('dp', 'col'), 'row')
- grad_gain_first: float32 [1024], P('row')
- grad_shift_first: float32 [1024], P('row')
- grad_w_query: float32 [1024, 1024], P('row', 'col')
- grad_w_key: float32 [1024, 1024], P('row', 'col')
- grad_w_value: float32 [1024, 1024], P('row', 'col')
- grad_w_output: float32 [1024, 1024], P('col', 'row')
- grad_gain_second: float32 [1024], P('row')
- grad_shift_second: float32 [1024], P('row')
- grad_w_up: float32 [1024, 4096], P('row', 'col')
- grad_bias_up: float32 [4096], P('col')
- grad_w_down: float32 [4096, 1024], P('col', 'row')
- grad_bias_down: float32 [1024], P('row')
Inputs may be any that keep to these rules, and one draw needn't show every extreme that they name: `segments`: each sequence of 1024 tokens holds four documents labelled 1, 2, 3, 4 in order, then 1 to 64 padding tokens labelled 0; each of the first three documents has 100 to 300 tokens. `global_blocks`: distinct block positions; one of them is the last block, 15.
All inputs are finite; a program needn't handle non-finite values.
Results may differ from a plain program's by a relative error of at most 0.015.
Values may be sent and summed in bfloat16 or wider, within the bound.
No kernel may reach another device: no remote copies, remote signals or barrier semaphores. Data moves between devices by JAX's collectives and lax.ppermute only.
A program may use at most 256 MiB of HBM per device.

v0:
```python
import math
import jax
import jax.numpy as jnp
from jax import lax
from jax.sharding import PartitionSpec as P

D = 1024
HD = 64
BLK = 64
NB = 16
EPS = 1e-05


def product(picked, weight, flipped):
    if flipped:
        return lax.dot_general(
            picked, weight, (((1,), (1,)), ((), ())), preferred_element_type=jnp.float32
        )
    return jnp.dot(picked, weight, preferred_element_type=jnp.float32)


def to_columns(moving, weight, flipped):
    gathered = lax.all_gather(moving, "col", axis=0, tiled=True)
    row_count = gathered.shape[0] // lax.axis_size("row")

    def term_rows(first_row, how_many):
        return product(gathered, weight, flipped)

    result = lax.psum_scatter(
        term_rows(jnp.int32(0), lax.axis_size("row") * row_count),
        "row",
        scatter_dimension=0,
        tiled=True,
    )
    return (result, gathered)


def to_rows(moving, weight, flipped):
    gathered = lax.all_gather(moving, "row", axis=0, tiled=True)
    row_count = gathered.shape[0] // lax.axis_size("col")

    def term_rows(first_row, how_many):
        return product(gathered, weight, flipped)

    return (
        lax.psum_scatter(
            term_rows(jnp.int32(0), lax.axis_size("col") * row_count),
            "col",
            scatter_dimension=0,
            tiled=True,
        ),
        gathered,
    )


def norm_sums(first_sum, second_sum):
    return lax.psum((first_sum, second_sum), "row")


def norm_forward(moving, gain_row, shift_row):
    totals, squares = norm_sums(jnp.sum(moving, axis=1), jnp.sum(moving * moving, axis=1))
    center = totals / D
    spread = squares / D - center * center
    inverse = lax.rsqrt(spread + EPS)
    normed = (moving - center[:, None]) * inverse[:, None]
    return (normed * gain_row + shift_row, normed, inverse)


def norm_backward(upstream, normed, inverse, gain_row):
    scaled = upstream * gain_row
    first_sum, second_sum = norm_sums(jnp.sum(scaled, axis=1), jnp.sum(scaled * normed, axis=1))
    return inverse[:, None] * (scaled - first_sum[:, None] / D - normed * (second_sum[:, None] / D))


def head_masks(random_blocks, global_blocks):
    block_ids = jnp.arange(NB, dtype=jnp.int32)
    nearby = jnp.abs(block_ids[:, None] - block_ids[None, :]) <= 1
    chosen = jnp.any(random_blocks[:, :, :, None] == block_ids[None, None, None, :], axis=2)
    marked = jnp.any(global_blocks[:, None] == block_ids[None, :], axis=0)
    block_table = nearby[None] | chosen | marked[None, None, :] | marked[None, :, None]
    return jnp.repeat(jnp.repeat(block_table, BLK, axis=1), BLK, axis=2)


def seq_logits(seq_queries, seq_keys, labels, pattern):
    same_doc = (labels[:, None] == labels[None, :]) & (labels[None, :] != 0)
    raw_scores = jnp.einsum(
        "qhd,khd->hqk", seq_queries, seq_keys, preferred_element_type=jnp.float32
    )
    return jnp.where(pattern & same_doc[None], raw_scores * (1.0 / math.sqrt(HD)), -1000000000.0)


def attend_forward(queries, key_block, value_block, segments, pattern):

    def one_seq(pieces):
        seq_queries, seq_keys, seq_values, labels = pieces
        logits = seq_logits(seq_queries, seq_keys, labels, pattern)
        row_peak = jnp.max(logits, axis=2, keepdims=True)
        exp_terms = jnp.exp(logits - row_peak)
        row_total = jnp.sum(exp_terms, axis=2, keepdims=True)
        softmax = (exp_terms / row_total).astype(jnp.bfloat16)
        attended = jnp.einsum(
            "hqk,khd->qhd", softmax, seq_values, preferred_element_type=jnp.float32
        )
        live_rows = (labels != 0).astype(jnp.float32)
        return (attended * live_rows[:, None, None], (row_peak + jnp.log(row_total))[:, :, 0])

    return lax.map(one_seq, (queries, key_block, value_block, segments))


def attend_backward(queries, key_block, value_block, segments, pattern, grad_heads, log_total):

    def one_seq(pieces):
        seq_queries, seq_keys, seq_values, labels, seq_grads, seq_log = pieces
        logits = seq_logits(seq_queries, seq_keys, labels, pattern)
        softmax = jnp.exp(logits - seq_log[:, :, None])
        grad_probs = jnp.einsum(
            "qhd,khd->hqk", seq_grads, seq_values, preferred_element_type=jnp.float32
        )
        grad_values = jnp.einsum(
            "hqk,qhd->khd",
            softmax.astype(jnp.bfloat16),
            seq_grads,
            preferred_element_type=jnp.float32,
        )
        inner_sum = jnp.sum(softmax * grad_probs, axis=2, keepdims=True)
        grad_raw = (softmax * (grad_probs - inner_sum) * (1.0 / math.sqrt(HD))).astype(jnp.bfloat16)
        grad_queries = jnp.einsum(
            "hqk,khd->qhd", grad_raw, seq_keys, preferred_element_type=jnp.float32
        )
        grad_keys = jnp.einsum(
            "hqk,qhd->khd", grad_raw, seq_queries, preferred_element_type=jnp.float32
        )
        return (grad_queries, grad_keys, grad_values)

    return lax.map(one_seq, (queries, key_block, value_block, segments, grad_heads, log_total))


def gelu_tanh(values):
    return jax.nn.gelu(values, approximate=True)


def weight_grad(left, right):
    return lax.dot_general(
        left, right, (((0,), (0,)), ((), ())), preferred_element_type=jnp.float32
    )


def body(
    inputs,
    gain_first,
    shift_first,
    w_query,
    w_key,
    w_value,
    w_output,
    gain_second,
    shift_second,
    w_up,
    bias_up,
    w_down,
    bias_down,
    segments,
    random_blocks,
    global_blocks,
    cotangent,
):
    seq_count, seq_len = segments.shape
    head_width = w_query.shape[1]
    heads_here = random_blocks.shape[0]
    seq_shape = (seq_count, seq_len, heads_here, HD)
    pattern = head_masks(random_blocks, global_blocks)
    live_tokens = (segments != 0).reshape(-1)
    x_first = inputs.astype(jnp.float32)
    first_full, normed_one, inverse_one = norm_forward(x_first, gain_first, shift_first)
    first_low = first_full.astype(jnp.bfloat16)
    stacked = jnp.concatenate((w_query, w_key, w_value), axis=1)
    projected, first_all = to_columns(first_low, stacked, False)
    proj_low = projected.astype(jnp.bfloat16)
    queries = proj_low[:, :head_width].reshape(seq_shape)
    key_block = proj_low[:, head_width : 2 * head_width].reshape(seq_shape)
    value_block = proj_low[:, 2 * head_width :].reshape(seq_shape)
    heads_out, log_total = attend_forward(queries, key_block, value_block, segments, pattern)
    heads_low = heads_out.reshape(-1, head_width).astype(jnp.bfloat16)
    mixed_out, heads_all = to_rows(heads_low, w_output, False)
    residual = x_first + mixed_out
    second_full, normed_two, inverse_two = norm_forward(residual, gain_second, shift_second)
    second_low = second_full.astype(jnp.bfloat16)
    upward, second_all = to_columns(second_low, w_up, False)
    upward = upward + bias_up
    hidden_low = gelu_tanh(upward).astype(jnp.bfloat16)
    downward, hidden_all = to_rows(hidden_low, w_down, False)
    layer_out = (residual + (downward + bias_down)).astype(jnp.bfloat16)
    grad_hidden, cotangent_all = to_columns(cotangent, w_down, True)
    activated, pull_back = jax.vjp(gelu_tanh, upward)
    grad_upward = pull_back(grad_hidden)[0].astype(jnp.bfloat16)
    grad_second, grad_upward_all = to_rows(grad_upward, w_up, True)
    grad_residual = cotangent.astype(jnp.float32) + norm_backward(
        grad_second, normed_two, inverse_two, gain_second
    )
    grad_mixed = grad_residual.astype(jnp.bfloat16)
    grad_heads, grad_mixed_all = to_columns(grad_mixed, w_output, True)
    grad_heads = jnp.where(live_tokens[:, None], grad_heads, 0.0).astype(jnp.bfloat16)
    grad_queries, grad_keys, grad_values = attend_backward(
        queries, key_block, value_block, segments, pattern, grad_heads.reshape(seq_shape), log_total
    )
    grad_proj = jnp.concatenate(
        (
            grad_queries.reshape(-1, head_width),
            grad_keys.reshape(-1, head_width),
            grad_values.reshape(-1, head_width),
        ),
        axis=1,
    ).astype(jnp.bfloat16)
    grad_first, grad_proj_all = to_rows(grad_proj, stacked, True)
    grad_inputs = grad_residual + norm_backward(grad_first, normed_one, inverse_one, gain_first)
    grad_stacked = weight_grad(first_all, grad_proj_all)
    grad_out_weight = weight_grad(heads_all, grad_mixed_all)
    grad_up_weight = weight_grad(second_all, grad_upward_all)
    grad_down_weight = weight_grad(hidden_all, cotangent_all)
    grad_up_bias = jnp.sum(grad_upward_all, axis=0, dtype=jnp.float32)
    grad_down_bias = jnp.sum(cotangent_all, axis=0, dtype=jnp.float32)
    gain_terms = lax.psum(
        (
            jnp.sum(grad_first * normed_one, axis=0),
            jnp.sum(grad_first, axis=0),
            jnp.sum(grad_second * normed_two, axis=0),
            jnp.sum(grad_second, axis=0),
        ),
        ("dp", "col"),
    )
    summed = (
        lax.psum(grad_stacked.astype(jnp.bfloat16), "dp").astype(jnp.float32),
        lax.psum(grad_out_weight.astype(jnp.bfloat16), "dp").astype(jnp.float32),
        lax.psum(grad_up_weight.astype(jnp.bfloat16), "dp").astype(jnp.float32),
        lax.psum(grad_down_weight.astype(jnp.bfloat16), "dp").astype(jnp.float32),
        lax.psum(grad_up_bias.astype(jnp.bfloat16), "dp").astype(jnp.float32),
        lax.psum(grad_down_bias.astype(jnp.bfloat16), "dp").astype(jnp.float32),
    )
    return (
        layer_out,
        grad_inputs,
        gain_terms[0],
        gain_terms[1],
        summed[0][:, :head_width],
        summed[0][:, head_width : 2 * head_width],
        summed[0][:, 2 * head_width :],
        summed[1],
        gain_terms[2],
        gain_terms[3],
        summed[2],
        summed[4],
        summed[3],
        summed[5],
    )


def solution(mesh):
    placed = (
        P(("dp", "col"), "row"),
        P("row"),
        P("row"),
        P("row", "col"),
        P("row", "col"),
        P("row", "col"),
        P("col", "row"),
        P("row"),
        P("row"),
        P("row", "col"),
        P("col"),
        P("col", "row"),
        P("row"),
        P(("dp", "row"), None),
        P("col", None, None),
        P(),
        P(("dp", "col"), "row"),
    )
    return jax.shard_map(
        body,
        mesh=mesh,
        in_specs=placed,
        out_specs=(
            P(("dp", "col"), "row"),
            P(("dp", "col"), "row"),
            P("row"),
            P("row"),
            P("row", "col"),
            P("row", "col"),
            P("row", "col"),
            P("col", "row"),
            P("row"),
            P("row"),
            P("row", "col"),
            P("col"),
            P("col", "row"),
            P("row"),
        ),
        check_vma=False,
    )
```

profile of v0, /device:TPU:0, one launch (start us, length us, event | category | flops | bytes accessed | tf_op | source)
XLA Modules:
  0.0 1793.3 jit_solution(9766734146856281676)
XLA Ops:
  7.3 2.0 convert_reduce_fusion
  9.2 12.7 all-reduce.4
  22.6 2.5 fusion.36
  25.3 33.4 %all-gather.9.cloned.1.call-done = bf16[4096,256]{1,0:T(8,128)(2,1)} async-done(((bf16[2048,256]{1,0:T(8,128)(2,1)}), bf16[4096,256]{1,0:T(8,128)(2,1)}) %all-gather.9.cloned.1.call-update) | async-done | bytes 2097168 | tf_op jit(solution)/shard_map/all_gather | solution.py:23
  58.7 11.8 fusion.66
  72.4 1.8 compare_and_fusion
  74.2 178.4 %reduce-scatter.9.cloned.1.call-done = f32[1024,1536]{1,0:T(8,128)} async-done(((f32[4096,1536]{1,0:T(8,128)}), f32[1024,1536]{1,0:T(8,128)}) %reduce-scatter.9.cloned.1.call-update) | async-done | bytes 6291472 | tf_op jit(solution)/shard_map/reduce_scatter | solution.py:29
  252.6 3.2 convert_element_type.96
  255.7 1.3 fusion.63
  257.0 2.3 copy.57
  259.3 1.3 copy.56
  261.1 16.7 fusion.65
  277.8 13.0 fusion.2
  290.8 14.6 multiply_convert_fusion.2
  305.5 34.5 %all-gather.11.cloned.1.call-done = bf16[4096,512]{0,1:T(8,128)(2,1)} async-done(((bf16[1024,512]{0,1:T(8,128)(2,1)}), bf16[4096,512]{0,1:T(8,128)(2,1)}) %all-gather.11.cloned.1.call-update) | async-done | bytes 4194320 | tf_op jit(solution)/shard_map/all_gather | solution.py:39
  340.1 5.5 fusion.67
  346.3 53.9 %reduce-scatter.11.cloned.1.call-done = f32[2048,256]{1,0:T(8,128)} async-done(((f32[4096,256]{1,0:T(8,128)}), f32[2048,256]{1,0:T(8,128)}) %reduce-scatter.11.cloned.1.call-update) | async-done | bytes 2097168 | tf_op jit(solution)/shard_map/reduce_scatter | solution.py:46
  400.2 2.5 fusion.61
  402.7 11.0 all-reduce.3
  413.6 1.5 add_convert_fusion.1
  415.2 19.5 %all-gather.17.cloned.1.call-done = bf16[4096,256]{1,0:T(8,128)(2,1)} async-done(((bf16[2048,256]{1,0:T(8,128)(2,1)}), bf16[4096,256]{1,0:T(8,128)(2,1)}) %all-gather.17.cloned.1.call-update) | async-done | bytes 2097168 | tf_op jit(solution)/shard_map/all_gather | solution.py:23
  434.7 18.6 %fusion.70 = f32[4096,2048]{1,0:T(8,128)} fusion(bf16[4096,256]{1,0:T(8,128)(2,1)} %all-gather.17.cloned.1.call-done, bf16[2048,256]{1,0:T(8,128)(2,1)} %param.28), kind=kOutput, calls=%fused_computation.97 | convolution fusion | flops 4294967296 | bytes 36700160 | tf_op jit(solution)/shard_map/dot_general | solution.py:16
  453.3 16.5 all-gather.13.cloned.1.call-done
  469.8 20.5 %fusion.68 = f32[4096,2048]{1,0:T(8,128)} fusion(bf16[4096,256]{1,0:T(8,128)(2,1)} %all-gather.13.cloned.1.call-done, bf16[256,2048]{1,0:T(8,128)(2,1)S(1)} %copy-done), kind=kOutput, calls=%fused_computation.95 | convolution fusion | flops 4294967296 | bytes 36700160 | tf_op jit(solution)/shard_map/dot_general | solution.py:19
  490.4 214.3 %reduce-scatter.17.cloned.1.call-done = f32[1024,2048]{1,0:T(8,128)} async-done(((f32[4096,2048]{1,0:T(8,128)}), f32[1024,2048]{1,0:T(8,128)}) %reduce-scatter.17.cloned.1.call-update) | async-done | bytes 8388624 | tf_op jit(solution)/shard_map/reduce_scatter | solution.py:29
  704.7 234.9 %reduce-scatter.13.cloned.1.call-done = f32[1024,2048]{1,0:T(8,128)} async-done(((f32[4096,2048]{1,0:T(8,128)}), f32[1024,2048]{1,0:T(8,128)}) %reduce-scatter.13.cloned.1.call-update) | async-done | bytes 8388624 | tf_op jit(solution)/shard_map/reduce_scatter | solution.py:29
  939.7 13.0 fusion.17
  953.7 105.0 %all-gather.19.cloned.1.call-done = bf16[4096,2048]{1,0:T(8,128)(2,1)} async-done(((bf16[1024,2048]{1,0:T(8,128)(2,1)}), bf16[4096,2048]{1,0:T(8,128)(2,1)}) %all-gather.19.cloned.1.call-update) | async-done | bytes 16777232 | tf_op jit(solution)/shard_map/all_gather | solution.py:39
  1058.8 10.3 fusion.71
  1069.2 96.9 %all-gather.15.cloned.1.call-done = bf16[4096,2048]{1,0:T(8,128)(2,1)} async-done(((bf16[1024,2048]{1,0:T(8,128)(2,1)}), bf16[4096,2048]{1,0:T(8,128)(2,1)}) %all-gather.15.cloned.1.call-update) | async-done | bytes 16777232 | tf_op jit(solution)/shard_map/all_gather | solution.py:39
  1166.1 10.1 fusion.69
  1176.3 46.5 %reduce-scatter.19.cloned.1.call-done = f32[2048,256]{1,0:T(8,128)} async-done(((f32[4096,256]{1,0:T(8,128)}), f32[2048,256]{1,0:T(8,128)}) %reduce-scatter.19.cloned.1.call-update) | async-done | bytes 2097168 | tf_op jit(solution)/shard_map/reduce_scatter | solution.py:46
  1222.8 2.5 multiply_reduce_fusion.1
  1225.3 11.1 all-reduce.2
  1236.5 42.9 %reduce-scatter.15.cloned.1.call-done = f32[2048,256]{1,0:T(8,128)} async-done(((f32[4096,256]{1,0:T(8,128)}), f32[2048,256]{1,0:T(8,128)}) %reduce-scatter.15.cloned.1.call-update) | async-done | bytes 2097168 | tf_op jit(solution)/shard_map/reduce_scatter | solution.py:46
  1279.4 5.8 fusion.62
  1285.3 33.2 %all-gather.21.cloned.1.call-done = bf16[4096,256]{1,0:T(8,128)(2,1)} async-done(((bf16[2048,256]{1,0:T(8,128)(2,1)}), bf16[4096,256]{1,0:T(8,128)(2,1)}) %all-gather.21.cloned.1.call-update) | async-done | bytes 2097168 | tf_op jit(solution)/shard_map/all_gather | solution.py:23
  1318.5 6.1 fusion.72
  1324.8 71.3 %reduce-scatter.21.cloned.1.call-done = f32[1024,512]{1,0:T(8,128)} async-done(((f32[4096,512]{1,0:T(8,128)}), f32[1024,512]{1,0:T(8,128)}) %reduce-scatter.21.cloned.1.call-update) | async-done | bytes 2097168 | tf_op jit(solution)/shard_map/reduce_scatter | solution.py:29
  1396.1 1.8 select_convert_fusion
  1398.5 31.5 %fusion.43 = bf16[8,64,1024]{2,1,0:T(8,128)(2,1)} fusion(bf16[1024,8,64]{0,2,1:T(8,128)(2,1)S(1)} %bitcast.68, f32[8,1024,1024]{1,2,0:T(8,128)} %get-tuple-element.118, f32[8,1024]{1,0:T(8,128)S(1)} %log_add_fusion, bf16[1024,8,64]{0,2,1:T(8,128)(2,1)S(1)} %bitcast.63, bf16[1024,8,64]{0,2,1:T(8,128)(2,1)} %bitcast.72), kind=kOutput, calls=%fused_computation.61 | convolution fusion | flops 3280479232 | bytes 37781504 | tf_op jit(solution)/shard_map/while/body/eval_jaxpr/hqk,khd->qhd/dot_general | solution.py:127
  1430.0 33.5 %fusion.48 = bf16[8,64,1024]{2,1,0:T(8,128)(2,1)} fusion(bf16[1024,8,64]{0,2,1:T(8,128)(2,1)S(1)} %bitcast.70, f32[8,1024,1024]{1,2,0:T(8,128)} %get-tuple-element.118, f32[8,1024]{1,0:T(8,128)S(1)} %log_add_fusion, bf16[1024,8,64]{0,2,1:T(8,128)(2,1)S(1)} %bitcast.64, bf16[1024,8,64]{0,2,1:T(8,128)(2,1)} %bitcast.73), kind=kOutput, calls=%fused_computation.62 | convolution fusion | flops 3280479232 | bytes 37781504 | tf_op jit(solution)/shard_map/while/body/eval_jaxpr/hqk,qhd->khd/dot_general | solution.py:130
  1463.5 13.5 fusion.53
  1477.0 2.9 pad_maximum_fusion
  1480.2 12.8 convolution_convert_fusion
  1493.0 10.3 convolution_convert_fusion.1
  1503.3 2.0 convolution_convert_fusion.3
  1505.3 56.8 %all-gather.23.cloned.1.call-done = bf16[4096,1536]{0,1:T(8,128)(2,1)} async-done(((bf16[1024,1536]{0,1:T(8,128)(2,1)}), bf16[4096,1536]{0,1:T(8,128)(2,1)}) %all-gather.23.cloned.1.call-update) | async-done | bytes 12582928 | tf_op jit(solution)/shard_map/all_gather | solution.py:39
  1562.1 7.5 convolution_convert_fusion.2
  1570.0 10.2 fusion.73
  1580.2 1.6 copy-done.4
  1582.3 9.8 reduce_sum.166
  1592.1 12.6 all-reduce.5
  1605.3 0.6 convert_element_type.117
  1605.9 85.5 %all-reduce.9.cloned.1.call-done = (bf16[256,1536]{1,0:T(8,128)(2,1)}, bf16[512,256]{1,0:T(8,128)(2,1)}, bf16[256,2048]{1,0:T(8,128)(2,1)}, bf16[2048,256]{1,0:T(8,128)(2,1)}) async-done(((bf16[256,1536]{1,0:T(8,128)(2,1)}, bf16[512,256]{1,0:T(8,128)(2,1)}, bf16[256,2048]{1,0:T(8,128)(2,1)}, bf16[2048,256]{1,0:T(8,128)(2,1)}), (bf16[256,1536]{1,0:T(8,128)(2,1)}, bf16[512,256]{1,0:T(8,128)(2,1)}, ...) | async-done | bytes 3145744 | tf_op jit(solution)/shard_map/psum | solution.py:232
  1691.4 1.9 convert_element_type.114
  1693.3 2.9 convert_element_type.116
  1696.2 1.5 convert_element_type.119
  1697.7 1.2 fusion.64
  1698.9 48.1 %reduce-scatter.23.cloned.1.call-done = f32[2048,256]{1,0:T(8,128)} async-done(((f32[4096,256]{1,0:T(8,128)}), f32[2048,256]{1,0:T(8,128)}) %reduce-scatter.23.cloned.1.call-update) | async-done | bytes 2097168 | tf_op jit(solution)/shard_map/reduce_scatter | solution.py:46
  1747.0 2.7 fusion.41
  1749.7 10.7 all-reduce.1
  1760.5 21.0 %all-reduce = (f32[256]{0:T(256)}, f32[256]{0:T(256)}, f32[256]{0:T(256)}, f32[256]{0:T(256)}) all-reduce(f32[256]{0:T(256)S(1)} %get-tuple-element.62, f32[256]{0:T(256)S(1)} %get-tuple-element.78, f32[256]{0:T(256)S(1)} %get-tuple-element.60, f32[256]{0:T(256)S(1)} %get-tuple-element.77), channel_id=1, replica_groups=mesh['dp'=4,'row'=4,'col'=2] {'dp','col'}, use_global_device_ids=true, to_apply=%region_30.31 | all-reduce | flops 1024 | bytes 8192 | tf_op jit(solution)/shard_map/psum | solution.py:222
  1781.5 5.0 fusion.40
  (128 shorter events, 7.9 us)
Async XLA Ops:
  7.2 462.6 %copy-start = (bf16[256,2048]{1,0:T(8,128)(2,1)S(1)}, bf16[256,2048]{1,0:T(8,128)(2,1)}, u32[]{:S(2)}) copy-start(bf16[256,2048]{1,0:T(8,128)(2,1)} %param.26) | copy-start | bytes 3145732
  7.2 18.0 %copy-start.19 = (bf16[256,512]{1,0:T(8,128)(2,1)S(1)}, bf16[256,512]{1,0:T(8,128)(2,1)}, u32[]{:S(2)}) copy-start(bf16[256,512]{1,0:T(8,128)(2,1)} %param.20) | copy-start | bytes 786436
  7.2 18.0 %copy-start.20 = (bf16[256,512]{1,0:T(8,128)(2,1)S(1)}, bf16[256,512]{1,0:T(8,128)(2,1)}, u32[]{:S(2)}) copy-start(bf16[256,512]{1,0:T(8,128)(2,1)} %param.21) | copy-start | bytes 786436
  7.2 18.1 %copy-start.21 = (bf16[256,512]{1,0:T(8,128)(2,1)S(1)}, bf16[256,512]{1,0:T(8,128)(2,1)}, u32[]{:S(2)}) copy-start(bf16[256,512]{1,0:T(8,128)(2,1)} %param.22) | copy-start | bytes 786436
  7.2 51.5 %all-gather.9.cloned.1.call-start = ((), (), s32[]{:S(2)}) async-start(), calls=%async_computation.8 | async-start | bytes 3145728 | tf_op jit(solution)/shard_map/all_gather | solution.py:23
  22.0 0.6 copy-start.22
  22.0 0.6 copy-start.24
  25.1 227.4 %reduce-scatter.9.cloned.1.call-start = ((), (), s32[]{:S(2)}) async-start(), calls=%async_computation.9 | async-start | bytes 31457280 | tf_op jit(solution)/shard_map/reduce_scatter | solution.py:29
  25.3 45.1 %copy-start.12 = (bf16[256,1536]{1,0:T(8,128)(2,1)}, bf16[256,1536]{1,0:T(8,128)(2,1)S(1)}, u32[]{:S(2)}) copy-start(bf16[256,1536]{1,0:T(8,128)(2,1)S(1)} %constant_dynamic-update-slice_fusion) | copy-start | bytes 2359300
  70.4 0.7 copy-start.27
  70.4 0.7 copy-start.35
  70.4 1.9 copy-start.26
  70.5 269.6 %all-gather.11.cloned.1.call-start = ((), (), s32[]{:S(2)}) async-start(), calls=%async_computation.10 | async-start | bytes 5242880 | tf_op jit(solution)/shard_map/all_gather | solution.py:39
  72.4 180.2 %copy-start.29 = (pred[1024]{0:T(1024)(128)(4,1)}, pred[1024]{0:T(1024)(128)(4,1)S(1)}, u32[]{:S(2)}) copy-start(pred[1024]{0:T(1024)(128)(4,1)S(1)} %compare_reduce_fusion) | copy-start | bytes 3076
  261.1 29.7 %copy-start.17 = (bf16[1024,512]{0,1:T(8,128)(2,1)}, bf16[1024,512]{0,1:T(8,128)(2,1)S(1)}, u32[]{:S(2)}) copy-start(bf16[1024,512]{0,1:T(8,128)(2,1)S(1)} %copy.53) | copy-start | bytes 3145732
  290.8 49.3 %copy-start.16 = (bf16[512,256]{1,0:T(8,128)(2,1)S(1)}, bf16[512,256]{1,0:T(8,128)(2,1)}, u32[]{:S(2)}) copy-start(bf16[512,256]{1,0:T(8,128)(2,1)} %param.23) | copy-start | bytes 786436
  305.5 94.7 %reduce-scatter.11.cloned.1.call-start = ((), (), s32[]{:S(2)}) async-start(), calls=%async_computation.11 | async-start | bytes 6291456 | tf_op jit(solution)/shard_map/reduce_scatter | solution.py:46
  345.6 68.0 %copy-start.28 = (f32[256]{0:T(256)S(1)}, f32[256]{0:T(256)}, u32[]{:S(2)}) copy-start(f32[256]{0:T(256)} %param.24) | copy-start | bytes 3076
  345.6 68.0 %copy-start.33 = (f32[256]{0:T(256)S(1)}, f32[256]{0:T(256)}, u32[]{:S(2)}) copy-start(f32[256]{0:T(256)} %param.25) | copy-start | bytes 3076
  345.7 89.0 %all-gather.17.cloned.1.call-start = ((), (), s32[]{:S(2)}) async-start(), calls=%async_computation.16 | async-start | bytes 3145728 | tf_op jit(solution)/shard_map/all_gather | solution.py:23
  346.2 123.5 %all-gather.13.cloned.1.call-start = ((), (), s32[]{:S(2)}) async-start(), calls=%async_computation.12 | async-start | bytes 3145728 | tf_op jit(solution)/shard_map/all_gather | solution.py:23
  415.2 289.6 %reduce-scatter.17.cloned.1.call-start = ((), (), s32[]{:S(2)}) async-start(), calls=%async_computation.17 | async-start | bytes 41943040 | tf_op jit(solution)/shard_map/reduce_scatter | solution.py:29
  453.3 486.4 %reduce-scatter.13.cloned.1.call-start = ((), (), s32[]{:S(2)}) async-start(), calls=%async_computation.13 | async-start | bytes 41943040 | tf_op jit(solution)/shard_map/reduce_scatter | solution.py:29
  490.3 449.4 %copy-start.32 = (f32[2048]{0:T(1024)S(1)}, f32[2048]{0:T(1024)}, u32[]{:S(2)}) copy-start(f32[2048]{0:T(1024)} %param.27) | copy-start | bytes 24580
  490.3 568.4 %all-gather.19.cloned.1.call-start = ((), (), s32[]{:S(2)}) async-start(), calls=%async_computation.18 | async-start | bytes 20971520 | tf_op jit(solution)/shard_map/all_gather | solution.py:39
  952.7 213.4 %all-gather.15.cloned.1.call-start = ((), (), s32[]{:S(2)}) async-start(), calls=%async_computation.14 | async-start | bytes 20971520 | tf_op jit(solution)/shard_map/all_gather | solution.py:39
  953.3 269.5 %reduce-scatter.19.cloned.1.call-start = ((), (), s32[]{:S(2)}) async-start(), calls=%async_computation.19 | async-start | bytes 6291456 | tf_op jit(solution)/shard_map/reduce_scatter | solution.py:46
  1069.1 97.0 %copy-start.14 = (bf16[2048,256]{1,0:T(8,128)(2,1)S(1)}, bf16[2048,256]{1,0:T(8,128)(2,1)}, u32[]{:S(2)}) copy-start(bf16[2048,256]{1,0:T(8,128)(2,1)} %param.28) | copy-start | bytes 3145732
  1069.1 210.2 %reduce-scatter.15.cloned.1.call-start = ((), (), s32[]{:S(2)}) async-start(), calls=%async_computation.15 | async-start | bytes 6291456 | tf_op jit(solution)/shard_map/reduce_scatter | solution.py:46
  1176.2 103.2 %copy-start.6 = (bf16[2048,256]{1,0:T(8,128)(2,1)S(1)}, bf16[2048,256]{1,0:T(8,128)(2,1)}, u32[]{:S(2)}) copy-start(bf16[2048,256]{1,0:T(8,128)(2,1)} %param.33) | copy-start | bytes 3145732
  1176.2 103.2 %copy-start.34 = (f32[256]{0:T(256)S(1)}, f32[256]{0:T(256)}, u32[]{:S(2)}) copy-start(f32[256]{0:T(256)} %param.29) | copy-start | bytes 3076
  1176.2 142.3 %all-gather.21.cloned.1.call-start = ((), (), s32[]{:S(2)}) async-start(), calls=%async_computation.20 | async-start | bytes 3145728 | tf_op jit(solution)/shard_map/all_gather | solution.py:23
  1285.2 110.9 %reduce-scatter.21.cloned.1.call-start = ((), (), s32[]{:S(2)}) async-start(), calls=%async_computation.21 | async-start | bytes 10485760 | tf_op jit(solution)/shard_map/reduce_scatter | solution.py:29
  1324.5 71.6 %copy-start.30 = (pred[1024]{0:T(1024)(128)(4,1)S(1)}, pred[1024]{0:T(1024)(128)(4,1)}, u32[]{:S(2)}) copy-start(pred[1024]{0:T(1024)(128)(4,1)} %copy-done.29) | copy-start | bytes 3076
  1324.6 73.9 %copy-start.7 = (bf16[1024,512]{0,1:T(8,128)(2,1)S(1)}, bf16[1024,512]{0,1:T(8,128)(2,1)}, u32[]{:S(2)}) copy-start(bf16[1024,512]{0,1:T(8,128)(2,1)} %copy.57) | copy-start | bytes 3145732
  1324.6 237.5 %all-gather.23.cloned.1.call-start = ((), (), s32[]{:S(2)}) async-start(), calls=%async_computation.22 | async-start | bytes 15728640 | tf_op jit(solution)/shard_map/all_gather | solution.py:39
  1398.5 31.5 %copy-start.8 = (bf16[1024,512]{0,1:T(8,128)(2,1)S(1)}, bf16[1024,512]{0,1:T(8,128)(2,1)}, u32[]{:S(2)}) copy-start(bf16[1024,512]{0,1:T(8,128)(2,1)} %copy.56) | copy-start | bytes 3145732
  1463.5 13.5 copy-start.18
  1479.9 13.1 copy-start.3
  1479.9 211.5 %all-reduce.9.cloned.1.call-start = ((), (), s32[]{:S(2)}) async-start(), calls=%async_computation.24 | async-start | bytes 6291456 | tf_op jit(solution)/shard_map/psum | solution.py:232
  1493.0 10.3 copy-start.5
  1493.0 10.3 copy-start.10
  1503.3 58.8 %copy-start.9 = (bf16[4096,256]{1,0:T(8,128)(2,1)S(1)}, bf16[4096,256]{1,0:T(8,128)(2,1)}, u32[]{:S(2)}) copy-start(bf16[4096,256]{1,0:T(8,128)(2,1)} %all-gather.9.cloned.1.call-done) | copy-start | bytes 6291460
  1505.3 64.6 %copy-start.13 = (bf16[256,1536]{1,0:T(8,128)(2,1)S(1)}, bf16[256,1536]{1,0:T(8,128)(2,1)}, u32[]{:S(2)}) copy-start(bf16[256,1536]{1,0:T(8,128)(2,1)} %copy-done.12) | copy-start | bytes 2359300
  1569.6 177.3 %reduce-scatter.23.cloned.1.call-start = ((), (), s32[]{:S(2)}) async-start(), calls=%async_computation.23 | async-start | bytes 6291456 | tf_op jit(solution)/shard_map/reduce_scatter | solution.py:46
  1580.2 1.6 copy-start.4
  1691.4 4.8 copy-start.15
  1691.4 6.3 copy-start.11
  1693.3 53.7 %copy-start.2 = (bf16[2048,256]{1,0:T(8,128)(2,1)S(1)}, bf16[2048,256]{1,0:T(8,128)(2,1)}, u32[]{:S(2)}) copy-start(bf16[2048,256]{1,0:T(8,128)(2,1)} %param.17) | copy-start | bytes 3145732
  1693.3 53.7 %copy-start.23 = (f32[2048]{0:T(1024)S(1)}, f32[2048]{0:T(1024)}, u32[]{:S(2)}) copy-start(f32[2048]{0:T(1024)} %copy-done.22) | copy-start | bytes 24580
  1693.3 53.7 %copy-start.25 = (f32[2048]{0:T(1024)S(1)}, f32[2048]{0:T(1024)}, u32[]{:S(2)}) copy-start(f32[2048]{0:T(1024)} %copy-done.24) | copy-start | bytes 24580
  1693.3 53.7 %copy-start.31 = (f32[256]{0:T(256)S(1)}, f32[256]{0:T(256)}, u32[]{:S(2)}) copy-start(f32[256]{0:T(256)} %param.18) | copy-start | bytes 3076
  1747.0 39.5 %copy-start.1 = (bf16[256,2048]{1,0:T(8,128)(2,1)S(1)}, bf16[256,2048]{1,0:T(8,128)(2,1)}, u32[]{:S(2)}) copy-start(bf16[256,2048]{1,0:T(8,128)(2,1)} %param.26) | copy-start | bytes 3145732
Sparse Core Ops, SparseCore 0:
  25.3 33.3 all-gather.8
  70.6 181.9 reduce-scatter.8
  305.6 34.4 all-gather.10
  345.8 54.3 reduce-scatter.10
  401.6 33.0 all-gather.16
  436.7 33.0 all-gather.12
  472.4 232.3 reduce-scatter.16
  707.3 232.3 reduce-scatter.12
  952.8 105.9 all-gather.18
  1060.2 105.8 all-gather.14
  1168.4 54.3 reduce-scatter.18
  1225.0 54.3 reduce-scatter.14
  1285.4 33.0 all-gather.20
  1324.7 71.3 reduce-scatter.20
  1480.0 82.0 all-gather.22
  1569.8 121.6 all-reduce.8
  1693.6 53.3 reduce-scatter.22
where the time goes:
time: 1800 us; the launch traced here: 1790 us
  waiting for transfers between devices  1370 us (76%)
  matrix products  235 us (13%)
  blocking collectives  79.2 us (4%)
  other arithmetic  78.4 us (4%)
    reduce_scatter x4, waiting for transfers between devices, to_columns(): lax.psum_scatter(term_rows(jnp.int32(0), lax.axis_size('row') * row_count...  699 us
    all_gather x4, waiting for transfers between devices, to_rows(): gathered = lax.all_gather(moving, 'row', axis=0, tiled=True)  293 us
    reduce_scatter x4, waiting for transfers between devices, to_rows(): lax.psum_scatter(term_rows(jnp.int32(0), lax.axis_size('col') * row_count...  191 us
    all_gather x4, waiting for transfers between devices, to_columns(): gathered = lax.all_gather(moving, 'col', axis=0, tiled=True)  103 us
    psum x1, waiting for transfers between devices, body(): lax.psum(grad_stacked.astype(jnp.bfloat16), 'dp').astype(jnp.float32)  85.5 us
    dot_general x4, matrix products, product(): return jnp.dot(picked, weight, preferred_element_type=jnp.float32)  47.9 us
    psum x4, blocking collectives, norm_sums(): return lax.psum((first_sum, second_sum), 'row')  45.5 us
    dot_general x4, matrix products, product(): lax.dot_general(picked, weight, (((1,), (1,)), ((), ())), preferred_eleme...  45.2 us
  transfers between devices with their start and end apart: 17, of which 17 were waited for; matrix products, arithmetic and copies ran while one was open for 7% of the time, Pallas kernels for 0%

commit v1 on v0

--- a/solution.py
+++ b/solution.py
@@ -36,7 +36,25 @@
 
 
 def to_rows(moving, weight, flipped):
-    gathered = lax.all_gather(moving, "row", axis=0, tiled=True)
+    built = lax.axis_size("row")
+    piece_next = lax.axis_index("row")
+    x_next, last, arr_next = (built, piece_next, moving.shape[0])
+    block_list = [(p, (p + 1) % x_next) for p in range(x_next)]
+    seen = [(p, (p - 1) % x_next) for p in range(x_next)]
+    gathered = jnp.zeros((*moving.shape[:0], x_next * arr_next, *moving.shape[1:]), moving.dtype)
+    gathered = lax.dynamic_update_slice_in_dim(gathered, moving, last * arr_next, axis=0)
+    frame_out = mat_out = moving
+    earlier = x_next // 2
+    for hop_no in range(1, earlier + 1):
+        frame_out = lax.ppermute(frame_out, "row", block_list)
+        gathered = lax.dynamic_update_slice_in_dim(
+            gathered, frame_out, (last - hop_no) % x_next * arr_next, axis=0
+        )
+        if hop_no < x_next - earlier:
+            mat_out = lax.ppermute(mat_out, "row", seen)
+            gathered = lax.dynamic_update_slice_in_dim(
+                gathered, mat_out, (last + hop_no) % x_next * arr_next, axis=0
+            )
     row_count = gathered.shape[0] // lax.axis_size("col")
 
     def term_rows(first_row, how_many):

time: 1800 us -> 1850 us (1.028)
  local copies, waits for them, and re-layouts: 10.8 us -> 64.4 us
    ppermute x0 -> x12, waiting for transfers between devices: none -> 350 us  [the longest x8 326 us: to_rows(): frame_out = lax.ppermute(frame_out, 'row', block_list)]
    all_gather x4 -> x0, waiting for transfers between devices: 293 us -> none  [to_rows(): gathered = lax.all_gather(moving, 'row', axis=0, tiled=True)]
    reduce_scatter x4, waiting for transfers between devices: 191 us -> 142 us  [to_rows(): lax.psum_scatter(term_rows(jnp.int32(0), lax.axis_size('col') * row_count...]
    dynamic_update_slice x0 -> x13, local copies, waits for them, and re-layouts: none -> 30.2 us  [the longest x8 19.6 us: to_rows(): lax.dynamic_update_slice_in_dim(gathered, frame_out, (last - hop_no) % x_...]
  transfers between devices with their start and end apart: 17 -> 25, of which waited for: 17 -> 21; matrix products, arithmetic and copies ran while one was open for 7% -> 8% of each run, Pallas kernels for 0% -> 0%
where the time goes in v1:
time: 1850 us
  waiting for transfers between devices  1380 us (75%)
  matrix products  222 us (12%)
  other arithmetic  83.3 us (5%)
  blocking collectives  78.4 us (4%)
  local copies, waits for them, and re-layouts  64.4 us (3%)
    reduce_scatter x4, waiting for transfers between devices, to_columns(): lax.psum_scatter(term_rows(jnp.int32(0), lax.axis_size('row') * row_count...  698 us
    ppermute x8, waiting for transfers between devices, to_rows(): frame_out = lax.ppermute(frame_out, 'row', block_list)  326 us
    reduce_scatter x4, waiting for transfers between devices, to_rows(): lax.psum_scatter(term_rows(jnp.int32(0), lax.axis_size('col') * row_count...  142 us
    all_gather x4, waiting for transfers between devices, to_columns(): gathered = lax.all_gather(moving, 'col', axis=0, tiled=True)  99.9 us
    psum x1, waiting for transfers between devices, body(): lax.psum(grad_stacked.astype(jnp.bfloat16), 'dp').astype(jnp.float32)  86.8 us
    dot_general x4, matrix products, product(): return jnp.dot(picked, weight, preferred_element_type=jnp.float32)  45.9 us
    psum x4, blocking collectives, norm_sums(): return lax.psum((first_sum, second_sum), 'row')  44.8 us
    dot_general x4, matrix products, product(): lax.dot_general(picked, weight, (((1,), (1,)), ((), ())), preferred_eleme...  41 us
  transfers between devices with their start and end apart: 25, of which 21 were waited for; matrix products, arithmetic and copies ran while one was open for 8% of the time, Pallas kernels for 0%

profile of v1, /device:TPU:0, one launch (start us, length us, event | category | flops | bytes accessed | tf_op | source)
XLA Modules:
  0.0 1848.0 jit_solution(4975989300616727920)
XLA Ops:
  9.2 12.7 all-reduce.4
  28.1 30.6 %all-gather.5.cloned.1.call-done = bf16[4096,256]{1,0:T(8,128)(2,1)} async-done(((bf16[2048,256]{1,0:T(8,128)(2,1)}), bf16[4096,256]{1,0:T(8,128)(2,1)}) %all-gather.5.cloned.1.call-update) | async-done | bytes 2097168 | tf_op jit(solution)/shard_map/all_gather | solution.py:23
  58.6 11.8 fusion.67
  74.1 178.4 %reduce-scatter.9.cloned.1.call-done = f32[1024,1536]{1,0:T(8,128)} async-done(((f32[4096,1536]{1,0:T(8,128)}), f32[1024,1536]{1,0:T(8,128)}) %reduce-scatter.9.cloned.1.call-update) | async-done | bytes 6291472 | tf_op jit(solution)/shard_map/reduce_scatter | solution.py:29
  252.5 3.2 convert_element_type.96
  261.0 16.3 fusion.66
  277.4 13.1 fusion.2
  290.5 13.6 multiply_convert_fusion.2
  306.0 23.1 %collective-permute-done = bf16[1024,512]{0,1:T(8,128)(2,1)S(1)} collective-permute-done((bf16[1024,512]{0,1:T(8,128)(2,1)S(1)}, bf16[1024,512]{0,1:T(8,128)(2,1)S(1)}, u32[]{:S(2)}, u32[]{:S(2)}) %collective-permute-start) | collective-permute-done | bytes 1048608 | tf_op jit(solution)/shard_map/ppermute | solution.py:49
  331.5 12.1 collective-permute-done.2
  346.9 3.4 fusion.68
  350.9 53.6 %reduce-scatter.11.cloned.1.call-done = f32[2048,256]{1,0:T(8,128)} async-done(((f32[4096,256]{1,0:T(8,128)}), f32[2048,256]{1,0:T(8,128)}) %reduce-scatter.11.cloned.1.call-update) | async-done | bytes 2097168 | tf_op jit(solution)/shard_map/reduce_scatter | solution.py:64
  407.0 10.8 all-reduce.3
  419.4 19.7 %all-gather.9.cloned.1.call-done = bf16[4096,256]{1,0:T(8,128)(2,1)} async-done(((bf16[2048,256]{1,0:T(8,128)(2,1)}), bf16[4096,256]{1,0:T(8,128)(2,1)}) %all-gather.9.cloned.1.call-update) | async-done | bytes 2097168 | tf_op jit(solution)/shard_map/all_gather | solution.py:23
  439.1 18.6 %fusion.71 = f32[4096,2048]{1,0:T(8,128)} fusion(bf16[4096,256]{1,0:T(8,128)(2,1)} %all-gather.9.cloned.1.call-done, bf16[2048,256]{1,0:T(8,128)(2,1)} %param.28), kind=kOutput, calls=%fused_computation.113 | convolution fusion | flops 4294967296 | bytes 36700160 | tf_op jit(solution)/shard_map/dot_general | solution.py:16
  457.7 16.5 all-gather.7.cloned.1.call-done
  474.2 20.7 %fusion.69 = f32[4096,2048]{1,0:T(8,128)} fusion(bf16[4096,256]{1,0:T(8,128)(2,1)} %all-gather.7.cloned.1.call-done, bf16[256,2048]{1,0:T(8,128)(2,1)S(1)} %copy-done), kind=kOutput, calls=%fused_computation.111 | convolution fusion | flops 4294967296 | bytes 36700160 | tf_op jit(solution)/shard_map/dot_general | solution.py:19
  495.4 213.6 %reduce-scatter.17.cloned.1.call-done = f32[1024,2048]{1,0:T(8,128)} async-done(((f32[4096,2048]{1,0:T(8,128)}), f32[1024,2048]{1,0:T(8,128)}) %reduce-scatter.17.cloned.1.call-update) | async-done | bytes 8388624 | tf_op jit(solution)/shard_map/reduce_scatter | solution.py:29
  709.0 234.9 %reduce-scatter.13.cloned.1.call-done = f32[1024,2048]{1,0:T(8,128)} async-done(((f32[4096,2048]{1,0:T(8,128)}), f32[1024,2048]{1,0:T(8,128)}) %reduce-scatter.13.cloned.1.call-update) | async-done | bytes 8388624 | tf_op jit(solution)/shard_map/reduce_scatter | solution.py:29
  946.0 9.5 constant_dynamic-update-slice_fusion.10
  957.3 90.5 %collective-permute-done.6 = bf16[1024,2048]{1,0:T(8,128)(2,1)S(1)} collective-permute-done((bf16[1024,2048]{1,0:T(8,128)(2,1)S(1)}, bf16[1024,2048]{1,0:T(8,128)(2,1)S(1)}, u32[]{:S(2)}, u32[]{:S(2)}) %collective-permute-start.6) | collective-permute-done | bytes 4194336 | tf_op jit(solution)/shard_map/ppermute | solution.py:49
  1047.8 6.0 broadcast.127.clone.1
  1053.8 7.2 constant_dynamic-update-slice_fusion.14
  1061.6 2.8 constant_dynamic-update-slice_fusion.8
  1064.4 31.4 %collective-permute-done.8 = bf16[1024,2048]{1,0:T(8,128)(2,1)} collective-permute-done((bf16[1024,2048]{1,0:T(8,128)(2,1)S(1)}, bf16[1024,2048]{1,0:T(8,128)(2,1)}, u32[]{:S(2)}, u32[]{:S(2)}) %collective-permute-start.8) | collective-permute-done | bytes 4194336 | tf_op jit(solution)/shard_map/ppermute | solution.py:49
  1095.8 2.8 constant_dynamic-update-slice_fusion.7
  1098.7 5.7 copy-done.2
  1104.4 6.2 fusion.72
  1110.7 59.3 %collective-permute-done.3 = bf16[1024,2048]{1,0:T(8,128)(2,1)} collective-permute-done((bf16[1024,2048]{1,0:T(8,128)(2,1)}, bf16[1024,2048]{1,0:T(8,128)(2,1)}, u32[]{:S(2)}, u32[]{:S(2)}) %collective-permute-start.3) | collective-permute-done | bytes 4194336 | tf_op jit(solution)/shard_map/ppermute | solution.py:49
  1170.0 4.7 constant_dynamic-update-slice_fusion.13
  1174.7 24.0 %collective-permute-done.4 = bf16[1024,2048]{1,0:T(8,128)(2,1)S(1)} collective-permute-done((bf16[1024,2048]{1,0:T(8,128)(2,1)}, bf16[1024,2048]{1,0:T(8,128)(2,1)S(1)}, u32[]{:S(2)}, u32[]{:S(2)}) %collective-permute-start.4) | collective-permute-done | bytes 4194336 | tf_op jit(solution)/shard_map/ppermute | solution.py:54
  1200.9 29.6 %collective-permute-done.5 = bf16[1024,2048]{1,0:T(8,128)(2,1)S(1)} collective-permute-done((bf16[1024,2048]{1,0:T(8,128)(2,1)}, bf16[1024,2048]{1,0:T(8,128)(2,1)S(1)}, u32[]{:S(2)}, u32[]{:S(2)}) %collective-permute-start.5) | collective-permute-done | bytes 4194336 | tf_op jit(solution)/shard_map/ppermute | solution.py:49
  1232.8 10.1 fusion.70
  1243.0 2.6 multiply_reduce_fusion.1
  1245.6 10.5 all-reduce.2
  1256.1 41.1 %reduce-scatter.15.cloned.1.call-done = f32[2048,256]{1,0:T(8,128)} async-done(((f32[4096,256]{1,0:T(8,128)}), f32[2048,256]{1,0:T(8,128)}) %reduce-scatter.15.cloned.1.call-update) | async-done | bytes 2097168 | tf_op jit(solution)/shard_map/reduce_scatter | solution.py:64
  1297.2 5.8 fusion.62
  1303.1 33.2 %all-gather.11.cloned.1.call-done = bf16[4096,256]{1,0:T(8,128)(2,1)} async-done(((bf16[2048,256]{1,0:T(8,128)(2,1)}), bf16[4096,256]{1,0:T(8,128)(2,1)}) %all-gather.11.cloned.1.call-update) | async-done | bytes 2097168 | tf_op jit(solution)/shard_map/all_gather | solution.py:23
  1336.4 6.1 fusion.73
  1342.5 71.5 %reduce-scatter.21.cloned.1.call-done = f32[1024,512]{1,0:T(8,128)} async-done(((f32[4096,512]{1,0:T(8,128)}), f32[1024,512]{1,0:T(8,128)}) %reduce-scatter.21.cloned.1.call-update) | async-done | bytes 2097168 | tf_op jit(solution)/shard_map/reduce_scatter | solution.py:29
  1416.6 13.5 fusion.53
  1430.1 33.7 %fusion.48 = bf16[8,64,1024]{2,1,0:T(8,128)(2,1)} fusion(bf16[1024,8,64]{0,2,1:T(8,128)(2,1)S(1)} %bitcast.70, f32[8,1024,1024]{1,2,0:T(8,128)} %get-tuple-element.122, f32[8,1024]{1,0:T(8,128)S(1)} %log_add_fusion, bf16[1024,8,64]{0,2,1:T(8,128)(2,1)S(1)} %bitcast.67, bf16[1024,8,64]{0,2,1:T(8,128)(2,1)} %bitcast.78), kind=kOutput, calls=%fused_computation.62 | convolution fusion | flops 3280479232 | bytes 37781504 | tf_op jit(solution)/shard_map/while/body/eval_jaxpr/hqk,qhd->khd/dot_general | solution.py:148
  1463.8 33.2 %fusion.43 = bf16[8,64,1024]{2,1,0:T(8,128)(2,1)} fusion(bf16[1024,8,64]{0,2,1:T(8,128)(2,1)} %bitcast.72, f32[8,1024,1024]{1,2,0:T(8,128)} %get-tuple-element.122, f32[8,1024]{1,0:T(8,128)S(1)} %log_add_fusion, bf16[1024,8,64]{0,2,1:T(8,128)(2,1)S(1)} %bitcast.68, bf16[1024,8,64]{0,2,1:T(8,128)(2,1)} %bitcast.79), kind=kOutput, calls=%fused_computation.61 | convolution fusion | flops 3280479232 | bytes 37781504 | tf_op jit(solution)/shard_map/while/body/eval_jaxpr/hqk,khd->qhd/dot_general | solution.py:145
  1497.0 6.1 broadcast_in_dim.59
  1503.1 3.0 pad_maximum_fusion
  1508.1 68.0 %collective-permute-done.9 = bf16[1024,1536]{0,1:T(8,128)(2,1)} collective-permute-done((bf16[1024,1536]{0,1:T(8,128)(2,1)}, bf16[1024,1536]{0,1:T(8,128)(2,1)}, u32[]{:S(2)}, u32[]{:S(2)}) %collective-permute-start.9) | collective-permute-done | bytes 3145760 | tf_op jit(solution)/shard_map/ppermute | solution.py:49
  1576.1 9.4 convolution_convert_fusion
  1585.6 5.5 convolution_convert_fusion.1
  1593.0 3.9 constant_dynamic-update-slice_fusion.5
  1596.9 4.0 constant_dynamic-update-slice_fusion.4
  1600.9 12.2 collective-permute-done.11
  1613.1 3.9 constant_dynamic-update-slice_fusion.3
  1617.0 7.5 convolution_convert_fusion.2
  1624.9 10.2 fusion.74
  1635.7 9.8 reduce_sum.166
  1645.5 12.6 all-reduce.5
  1659.3 86.8 %all-reduce.9.cloned.1.call-done = (bf16[256,1536]{1,0:T(8,128)(2,1)}, bf16[512,256]{1,0:T(8,128)(2,1)}, bf16[256,2048]{1,0:T(8,128)(2,1)}, bf16[2048,256]{1,0:T(8,128)(2,1)}) async-done(((bf16[256,1536]{1,0:T(8,128)(2,1)}, bf16[512,256]{1,0:T(8,128)(2,1)}, bf16[256,2048]{1,0:T(8,128)(2,1)}, bf16[2048,256]{1,0:T(8,128)(2,1)}), (bf16[256,1536]{1,0:T(8,128)(2,1)}, bf16[512,256]{1,0:T(8,128)(2,1)}, ...) | async-done | bytes 3145744 | tf_op jit(solution)/shard_map/psum | solution.py:250
  1747.9 2.8 convert_element_type.116
  1750.7 2.7 convert_element_type.119
  1754.6 47.2 %reduce-scatter.23.cloned.1.call-done = f32[2048,256]{1,0:T(8,128)} async-done(((f32[4096,256]{1,0:T(8,128)}), f32[2048,256]{1,0:T(8,128)}) %reduce-scatter.23.cloned.1.call-update) | async-done | bytes 2097168 | tf_op jit(solution)/shard_map/reduce_scatter | solution.py:64
  1801.8 2.6 fusion.41
  1804.4 10.7 all-reduce.1
  1815.2 21.0 %all-reduce = (f32[256]{0:T(256)}, f32[256]{0:T(256)}, f32[256]{0:T(256)}, f32[256]{0:T(256)}) all-reduce(f32[256]{0:T(256)S(1)} %get-tuple-element.62, f32[256]{0:T(256)S(1)} %get-tuple-element.78, f32[256]{0:T(256)S(1)} %get-tuple-element.60, f32[256]{0:T(256)S(1)} %get-tuple-element.77), channel_id=1, replica_groups=mesh['dp'=4,'row'=4,'col'=2] {'dp','col'}, use_global_device_ids=true, to_apply=%region_30.31 | all-reduce | flops 1024 | bytes 8192 | tf_op jit(solution)/shard_map/psum | solution.py:240
  1836.2 5.0 fusion.40
  (165 shorter events, 50.6 us)
Async XLA Ops:
  7.2 467.0 %copy-start = (bf16[256,2048]{1,0:T(8,128)(2,1)S(1)}, bf16[256,2048]{1,0:T(8,128)(2,1)}, u32[]{:S(2)}) copy-start(bf16[256,2048]{1,0:T(8,128)(2,1)} %param.26) | copy-start | bytes 3145732
  7.2 51.4 %all-gather.5.cloned.1.call-start = ((), (), s32[]{:S(2)}) async-start(), calls=%async_computation.8 | async-start | bytes 3145728 | tf_op jit(solution)/shard_map/all_gather | solution.py:23
  21.9 0.6 copy-start.21
  21.9 0.6 copy-start.23
  25.1 227.5 %reduce-scatter.9.cloned.1.call-start = ((), (), s32[]{:S(2)}) async-start(), calls=%async_computation.9 | async-start | bytes 31457280 | tf_op jit(solution)/shard_map/reduce_scatter | solution.py:29
  28.0 42.4 %copy-start.14 = (bf16[256,1536]{1,0:T(8,128)(2,1)}, bf16[256,1536]{1,0:T(8,128)(2,1)S(1)}, u32[]{:S(2)}) copy-start(bf16[256,1536]{1,0:T(8,128)(2,1)S(1)} %constant_dynamic-update-slice_fusion) | copy-start | bytes 2359300
  70.4 0.7 copy-start.27
  70.4 0.7 copy-start.34
  70.4 1.9 copy-start.25
  70.4 334.1 %reduce-scatter.11.cloned.1.call-start = ((), (), s32[]{:S(2)}) async-start(), calls=%async_computation.10 | async-start | bytes 6291456 | tf_op jit(solution)/shard_map/reduce_scatter | solution.py:64
  72.3 180.2 %copy-start.29 = (pred[1024]{0:T(1024)(128)(4,1)}, pred[1024]{0:T(1024)(128)(4,1)S(1)}, u32[]{:S(2)}) copy-start(pred[1024]{0:T(1024)(128)(4,1)S(1)} %compare_reduce_fusion) | copy-start | bytes 3076
  261.0 16.4 copy-start.10
  277.4 13.1 copy-start.20
  304.2 24.9 %collective-permute-start = (bf16[1024,512]{0,1:T(8,128)(2,1)S(1)}, bf16[1024,512]{0,1:T(8,128)(2,1)S(1)}, u32[]{:S(2)}, u32[]{:S(2)}) collective-permute-start(bf16[1024,512]{0,1:T(8,128)(2,1)S(1)} %bitcast.75), channel_id=1, source_target_pairs={{0,2},{2,4},{4,6},{6,0},{1,3},{3,5},{5,7},{7,1},{8,10},{10,12},{12... | collective-permute-start | bytes 3145736 | tf_op jit(solution)/shard_map/ppermute | solution.py:49
  304.3 25.9 %collective-permute-start.1 = (bf16[1024,512]{0,1:T(8,128)(2,1)S(1)}, bf16[1024,512]{0,1:T(8,128)(2,1)}, u32[]{:S(2)}, u32[]{:S(2)}) collective-permute-start(bf16[1024,512]{0,1:T(8,128)(2,1)S(1)} %bitcast.76), channel_id=1, source_target_pairs={{0,6},{2,0},{4,2},{6,4},{1,7},{3,1},{5,3},{7,5},{8,14},{10,8},{12,... | collective-permute-start | bytes 3145736 | tf_op jit(solution)/shard_map/ppermute | solution.py:54
  329.1 14.5 collective-permute-start.2
  329.3 17.6 copy-start.19
  344.9 2.0 copy-start.4
  350.3 67.5 %copy-start.28 = (f32[256]{0:T(256)S(1)}, f32[256]{0:T(256)}, u32[]{:S(2)}) copy-start(f32[256]{0:T(256)} %param.24) | copy-start | bytes 3076
  350.3 67.5 %copy-start.32 = (f32[256]{0:T(256)S(1)}, f32[256]{0:T(256)}, u32[]{:S(2)}) copy-start(f32[256]{0:T(256)} %param.25) | copy-start | bytes 3076
  350.3 88.8 %all-gather.9.cloned.1.call-start = ((), (), s32[]{:S(2)}) async-start(), calls=%async_computation.14 | async-start | bytes 3145728 | tf_op jit(solution)/shard_map/all_gather | solution.py:23
  350.9 123.3 %all-gather.7.cloned.1.call-start = ((), (), s32[]{:S(2)}) async-start(), calls=%async_computation.11 | async-start | bytes 3145728 | tf_op jit(solution)/shard_map/all_gather | solution.py:23
  419.3 289.6 %reduce-scatter.17.cloned.1.call-start = ((), (), s32[]{:S(2)}) async-start(), calls=%async_computation.15 | async-start | bytes 41943040 | tf_op jit(solution)/shard_map/reduce_scatter | solution.py:29
  457.7 486.3 %reduce-scatter.13.cloned.1.call-start = ((), (), s32[]{:S(2)}) async-start(), calls=%async_computation.12 | async-start | bytes 41943040 | tf_op jit(solution)/shard_map/reduce_scatter | solution.py:29
  494.9 451.1 %copy-start.26 = (f32[2048]{0:T(1024)S(1)}, f32[2048]{0:T(1024)}, u32[]{:S(2)}) copy-start(f32[2048]{0:T(1024)} %param.27) | copy-start | bytes 24580
  494.9 748.0 %reduce-scatter.19.cloned.1.call-start = ((), (), s32[]{:S(2)}) async-start(), calls=%async_computation.16 | async-start | bytes 6291456 | tf_op jit(solution)/shard_map/reduce_scatter | solution.py:64
  955.5 92.3 %collective-permute-start.6 = (bf16[1024,2048]{1,0:T(8,128)(2,1)S(1)}, bf16[1024,2048]{1,0:T(8,128)(2,1)S(1)}, u32[]{:S(2)}, u32[]{:S(2)}) collective-permute-start(bf16[1024,2048]{1,0:T(8,128)(2,1)S(1)} %get-tuple-element.104), channel_id=1, source_target_pairs={{0,2},{2,4},{4,6},{6,0},{1,3},{3,5},{5,7},{7,1},{8,10},{10,12},{12... | collective-permute-start | bytes 12582920 | tf_op jit(solution)/shard_map/ppermute | solution.py:49
  955.6 106.0 %collective-permute-start.7 = (bf16[1024,2048]{1,0:T(8,128)(2,1)S(1)}, bf16[1024,2048]{1,0:T(8,128)(2,1)}, u32[]{:S(2)}, u32[]{:S(2)}) collective-permute-start(bf16[1024,2048]{1,0:T(8,128)(2,1)S(1)} %get-tuple-element.104), channel_id=1, source_target_pairs={{0,6},{2,0},{4,2},{6,4},{1,7},{3,1},{5,3},{7,5},{8,14},{10,8},{12,... | collective-permute-start | bytes 12582920 | tf_op jit(solution)/shard_map/ppermute | solution.py:54
  1047.8 48.0 %collective-permute-start.8 = (bf16[1024,2048]{1,0:T(8,128)(2,1)S(1)}, bf16[1024,2048]{1,0:T(8,128)(2,1)}, u32[]{:S(2)}, u32[]{:S(2)}) collective-permute-start(bf16[1024,2048]{1,0:T(8,128)(2,1)S(1)} %collective-permute-done.6), channel_id=1, source_target_pairs={{0,2},{2,4},{4,6},{6,0},{1,3},{3,5},{5,7},{7,1},{8,10},{10,12},{12... | collective-permute-start | bytes 12582920 | tf_op jit(solution)/shard_map/ppermute | solution.py:49
  1061.0 109.0 %collective-permute-start.3 = (bf16[1024,2048]{1,0:T(8,128)(2,1)}, bf16[1024,2048]{1,0:T(8,128)(2,1)}, u32[]{:S(2)}, u32[]{:S(2)}) collective-permute-start(bf16[1024,2048]{1,0:T(8,128)(2,1)} %get-tuple-element.106), channel_id=1, source_target_pairs={{0,2},{2,4},{4,6},{6,0},{1,3},{3,5},{5,7},{7,1},{8,10},{10,12},{12... | collective-permute-start | bytes 12582920 | tf_op jit(solution)/shard_map/ppermute | solution.py:49
  1098.7 5.7 copy-start.2
  1110.6 186.7 %reduce-scatter.15.cloned.1.call-start = ((), (), s32[]{:S(2)}) async-start(), calls=%async_computation.13 | async-start | bytes 6291456 | tf_op jit(solution)/shard_map/reduce_scatter | solution.py:64
  1110.6 88.0 %collective-permute-start.4 = (bf16[1024,2048]{1,0:T(8,128)(2,1)}, bf16[1024,2048]{1,0:T(8,128)(2,1)S(1)}, u32[]{:S(2)}, u32[]{:S(2)}) collective-permute-start(bf16[1024,2048]{1,0:T(8,128)(2,1)} %get-tuple-element.106), channel_id=1, source_target_pairs={{0,6},{2,0},{4,2},{6,4},{1,7},{3,1},{5,3},{7,5},{8,14},{10,8},{12,... | collective-permute-start | bytes 12582920 | tf_op jit(solution)/shard_map/ppermute | solution.py:54
  1170.0 60.6 %collective-permute-start.5 = (bf16[1024,2048]{1,0:T(8,128)(2,1)}, bf16[1024,2048]{1,0:T(8,128)(2,1)S(1)}, u32[]{:S(2)}, u32[]{:S(2)}) collective-permute-start(bf16[1024,2048]{1,0:T(8,128)(2,1)} %collective-permute-done.3), channel_id=1, source_target_pairs={{0,2},{2,4},{4,6},{6,0},{1,3},{3,5},{5,7},{7,1},{8,10},{10,12},{12... | collective-permute-start | bytes 12582920 | tf_op jit(solution)/shard_map/ppermute | solution.py:49
  1200.9 31.9 %copy-start.16 = (bf16[2048,256]{1,0:T(8,128)(2,1)S(1)}, bf16[2048,256]{1,0:T(8,128)(2,1)}, u32[]{:S(2)}) copy-start(bf16[2048,256]{1,0:T(8,128)(2,1)} %param.28) | copy-start | bytes 3145732
  1242.9 54.4 %copy-start.8 = (bf16[2048,256]{1,0:T(8,128)(2,1)S(1)}, bf16[2048,256]{1,0:T(8,128)(2,1)}, u32[]{:S(2)}) copy-start(bf16[2048,256]{1,0:T(8,128)(2,1)} %param.33) | copy-start | bytes 3145732
  1242.9 54.4 %copy-start.33 = (f32[256]{0:T(256)S(1)}, f32[256]{0:T(256)}, u32[]{:S(2)}) copy-start(f32[256]{0:T(256)} %param.29) | copy-start | bytes 3076
  1242.9 93.5 %all-gather.11.cloned.1.call-start = ((), (), s32[]{:S(2)}) async-start(), calls=%async_computation.17 | async-start | bytes 3145728 | tf_op jit(solution)/shard_map/all_gather | solution.py:23
  1303.1 111.0 %reduce-scatter.21.cloned.1.call-start = ((), (), s32[]{:S(2)}) async-start(), calls=%async_computation.18 | async-start | bytes 10485760 | tf_op jit(solution)/shard_map/reduce_scatter | solution.py:29
  1342.5 71.6 %copy-start.30 = (pred[1024]{0:T(1024)(128)(4,1)S(1)}, pred[1024]{0:T(1024)(128)(4,1)}, u32[]{:S(2)}) copy-start(pred[1024]{0:T(1024)(128)(4,1)} %copy-done.29) | copy-start | bytes 3076
  1342.5 403.6 %all-reduce.9.cloned.1.call-start = ((), (), s32[]{:S(2)}) async-start(), calls=%async_computation.20 | async-start | bytes 6291456 | tf_op jit(solution)/shard_map/psum | solution.py:250
  1416.6 13.5 copy-start.9
  1497.0 6.1 copy-start.17
  1497.0 6.1 copy-start.18
  1503.1 73.0 %copy-start.7 = (bf16[4096,256]{1,0:T(8,128)(2,1)S(1)}, bf16[4096,256]{1,0:T(8,128)(2,1)}, u32[]{:S(2)}) copy-start(bf16[4096,256]{1,0:T(8,128)(2,1)} %all-gather.9.cloned.1.call-done) | copy-start | bytes 6291460
  1506.1 79.4 %slice-start = ((s8[16777216]{0:T(1024)(128)(4,1)}), s8[4194304]{0:T(1024)(128)(4,1)S(1)}, s32[]{:S(2)}) async-start(s8[16777216]{0:T(1024)(128)(4,1)} %bitcast.63), calls=%async_computation.21 | async-start | bytes 8388608
  1506.1 79.4 %slice-start.1 = ((s8[16777216]{0:T(1024)(128)(4,1)}), s8[4194304]{0:T(1024)(128)(4,1)S(1)}, s32[]{:S(2)}) async-start(s8[16777216]{0:T(1024)(128)(4,1)} %bitcast.63), calls=%async_computation.22 | async-start | bytes 8388608
  1506.1 79.4 %slice-start.2 = ((s8[16777216]{0:T(1024)(128)(4,1)}), s8[4194304]{0:T(1024)(128)(4,1)S(1)}, s32[]{:S(2)}) async-start(s8[16777216]{0:T(1024)(128)(4,1)} %bitcast.63), calls=%async_computation.23 | async-start | bytes 8388608
  1506.1 79.4 %slice-start.3 = ((s8[16777216]{0:T(1024)(128)(4,1)}), s8[4194304]{0:T(1024)(128)(4,1)S(1)}, s32[]{:S(2)}) async-start(s8[16777216]{0:T(1024)(128)(4,1)} %bitcast.63), calls=%async_computation.24 | async-start | bytes 8388608
  1506.1 79.5 %copy-start.6 = (bf16[4096,256]{1,0:T(8,128)(2,1)S(1)}, bf16[4096,256]{1,0:T(8,128)(2,1)}, u32[]{:S(2)}) copy-start(bf16[4096,256]{1,0:T(8,128)(2,1)} %all-gather.7.cloned.1.call-done) | copy-start | bytes 6291460
  1506.1 70.0 %collective-permute-start.9 = (bf16[1024,1536]{0,1:T(8,128)(2,1)}, bf16[1024,1536]{0,1:T(8,128)(2,1)}, u32[]{:S(2)}, u32[]{:S(2)}) collective-permute-start(bf16[1024,1536]{0,1:T(8,128)(2,1)} %get-tuple-element.108), channel_id=1, source_target_pairs={{0,2},{2,4},{4,6},{6,0},{1,3},{3,5},{5,7},{7,1},{8,10},{10,12},{12... | collective-permute-start | bytes 9437192 | tf_op jit(solution)/shard_map/ppermute | solution.py:49
  1506.2 90.8 %collective-permute-start.10 = (bf16[1024,1536]{0,1:T(8,128)(2,1)}, bf16[1024,1536]{0,1:T(8,128)(2,1)}, u32[]{:S(2)}, u32[]{:S(2)}) collective-permute-start(bf16[1024,1536]{0,1:T(8,128)(2,1)} %get-tuple-element.108), channel_id=1, source_target_pairs={{0,6},{2,0},{4,2},{6,4},{1,7},{3,1},{5,3},{7,5},{8,14},{10,8},{12,... | collective-permute-start | bytes 9437192 | tf_op jit(solution)/shard_map/ppermute | solution.py:54
  1576.1 37.0 %collective-permute-start.11 = (bf16[1024,1536]{0,1:T(8,128)(2,1)}, bf16[1024,1536]{0,1:T(8,128)(2,1)}, u32[]{:S(2)}, u32[]{:S(2)}) collective-permute-start(bf16[1024,1536]{0,1:T(8,128)(2,1)} %collective-permute-done.9), channel_id=1, source_target_pairs={{0,2},{2,4},{4,6},{6,0},{1,3},{3,5},{5,7},{7,1},{8,10},{10,12},{12... | collective-permute-start | bytes 9437192 | tf_op jit(solution)/shard_map/ppermute | solution.py:49
  1585.6 5.5 copy-start.5
  1585.6 5.5 copy-start.12
  1596.9 20.1 %copy-start.11 = (bf16[4096,256]{1,0:T(8,128)(2,1)S(1)}, bf16[4096,256]{1,0:T(8,128)(2,1)}, u32[]{:S(2)}) copy-start(bf16[4096,256]{1,0:T(8,128)(2,1)} %all-gather.5.cloned.1.call-done) | copy-start | bytes 6291460
  1617.0 7.9 copy-start.15
  1624.6 177.2 %reduce-scatter.23.cloned.1.call-start = ((), (), s32[]{:S(2)}) async-start(), calls=%async_computation.19 | async-start | bytes 6291456 | tf_op jit(solution)/shard_map/reduce_scatter | solution.py:64
  1645.4 156.4 %copy-start.3 = (bf16[2048,256]{1,0:T(8,128)(2,1)S(1)}, bf16[2048,256]{1,0:T(8,128)(2,1)}, u32[]{:S(2)}) copy-start(bf16[2048,256]{1,0:T(8,128)(2,1)} %param.17) | copy-start | bytes 3145732
  1645.4 156.4 %copy-start.22 = (f32[2048]{0:T(1024)S(1)}, f32[2048]{0:T(1024)}, u32[]{:S(2)}) copy-start(f32[2048]{0:T(1024)} %copy-done.21) | copy-start | bytes 24580
  1645.5 156.4 %copy-start.24 = (f32[2048]{0:T(1024)S(1)}, f32[2048]{0:T(1024)}, u32[]{:S(2)}) copy-start(f32[2048]{0:T(1024)} %copy-done.23) | copy-start | bytes 24580
  1645.5 156.3 %copy-start.31 = (f32[256]{0:T(256)S(1)}, f32[256]{0:T(256)}, u32[]{:S(2)}) copy-start(f32[256]{0:T(256)} %param.18) | copy-start | bytes 3076
  1746.1 7.3 copy-start.13
  1753.4 87.8 %copy-start.1 = (bf16[256,2048]{1,0:T(8,128)(2,1)S(1)}, bf16[256,2048]{1,0:T(8,128)(2,1)}, u32[]{:S(2)}) copy-start(bf16[256,2048]{1,0:T(8,128)(2,1)} %param.26) | copy-start | bytes 3145732
Sparse Core Ops, SparseCore 0:
  25.2 33.3 all-gather.4
  70.6 181.9 reduce-scatter.8
  350.4 54.0 reduce-scatter.10
  406.0 33.0 all-gather.8
  441.1 33.0 all-gather.6
  476.6 232.3 reduce-scatter.16
  711.6 232.3 reduce-scatter.12
  1110.7 54.1 reduce-scatter.18
  1243.0 54.1 reduce-scatter.14
  1303.2 33.0 all-gather.10
  1342.6 71.4 reduce-scatter.20
  1624.7 121.3 all-reduce.8
  1748.4 53.3 reduce-scatter.22
